TPU v7x, 32 devices: a whole 2x2x4 slice. The times are simulated.
32 devices in a mesh: pr: 4 (over y, x), pc: 8 (over z, core).
Axes of the slice: x: 2, y: 2, z: 4, core: 2. Of those that a mesh axis runs over, the one named last changes fastest.
Arguments:
- pair_state: bfloat16 [96, 96, 128], P('pr', 'pc'), may hold values from -6 to 6
- left_weight: bfloat16 [128, 128], replicated, may hold values from -0.5 to 0.5
- right_weight: bfloat16 [128, 128], replicated, may hold values from -0.5 to 0.5
- mid_gain: float32 [128], replicated, may hold values from 0.25 to 1.75
- out_weight: bfloat16 [128, 128], replicated, may hold values from -0.5 to 0.5
- out_gate: bfloat16 [128, 128], replicated, may hold values from -0.5 to 0.5
Outputs:
- pair_update: bfloat16 [96, 96, 128], P('pr', 'pc')
All inputs are finite; a program needn't handle non-finite values.
Results may differ from a plain program's by a relative error of at most 0.012.
Values may be sent and summed in bfloat16 or wider, within the bound.
A program may use at most 128 MiB of HBM per device.

v0:
```python
import jax
import jax.numpy as jnp
from jax import lax
from jax.sharding import PartitionSpec as P


def scale_channels(values, channel_gain):
    centred = values - jnp.mean(values, axis=-1, keepdims=True)
    return (
        centred
        * lax.rsqrt(jnp.mean(centred * centred, axis=-1, keepdims=True) + 1e-05)
        * channel_gain
    )


def project_pair(pair_in, left_weight, right_weight):
    left = jnp.einsum("ijc,cd->ijd", pair_in, left_weight, preferred_element_type=jnp.float32)
    right = jnp.einsum("ijc,cd->ijd", pair_in, right_weight, preferred_element_type=jnp.float32)
    return (pair_in, left.astype(jnp.bfloat16), right.astype(jnp.bfloat16))


def close_update(mixed, ready, mid_gain, out_weight, out_gate):
    scaled = scale_channels(mixed.astype(jnp.float32), mid_gain).astype(jnp.bfloat16)
    scaled = lax.optimization_barrier(scaled)
    gate = jax.nn.sigmoid(
        jnp.einsum("ijc,cd->ijd", ready, out_gate, preferred_element_type=jnp.float32)
    )
    return (
        jnp.einsum("ijd,dc->ijc", scaled, out_weight, preferred_element_type=jnp.float32) * gate
    ).astype(jnp.bfloat16)


def body(pair_state, left_weight, right_weight, mid_gain, out_weight, out_gate):
    ready, left, right = project_pair(pair_state, left_weight, right_weight)
    count = pair_state.shape[0] * lax.axis_size("pr")
    left_lines, right_lines = (
        lax.all_to_all(left, "pr", split_axis=2, concat_axis=0, tiled=True),
        lax.all_to_all(right, "pr", split_axis=2, concat_axis=0, tiled=True),
    )
    strip = jnp.einsum(
        "kid,kjd->ijd",
        lax.all_gather(left_lines, "pc", axis=1, tiled=True),
        right_lines,
        preferred_element_type=jnp.float32,
    )
    strip = (strip * count ** (-0.5)).astype(jnp.bfloat16)
    mixed = lax.all_to_all(strip, "pr", split_axis=0, concat_axis=2, tiled=True)
    return close_update(mixed, ready, mid_gain, out_weight, out_gate)


def solution(mesh):
    placed = (P("pr", "pc", None), P(), P(), P(), P(), P())
    return jax.shard_map(
        body, mesh=mesh, in_specs=placed, out_specs=P("pr", "pc", None), check_vma=False
    )
```

profile of v0, /device:TPU:0, one launch (start us, length us, event | category | flops | bytes accessed | tf_op | source)
XLA Modules:
  0.0 52.5 jit_solution(6551884356601724737)
XLA Ops:
  0.0 0.0 copy-start
  0.0 0.9 %copy-done = bf16[24,12,128]{2,0,1:T(8,128)(2,1)S(1)} copy-done((bf16[24,12,128]{2,0,1:T(8,128)(2,1)S(1)}, bf16[24,12,128]{2,0,1:T(8,128)(2,1)}, u32[]{:S(2)}) %copy-start) | copy-done | bytes 73752
  0.9 0.9 %convolution_convert_fusion.1 = bf16[24,12,128]{2,0,1:T(8,128)(2,1)S(1)} fusion(bf16[24,12,128]{2,0,1:T(8,128)(2,1)S(1)} %copy-done, bf16[128,128]{1,0:T(8,128)(2,1)} %param.8), kind=kOutput, calls=%fused_computation.10 | convolution fusion | flops 9474048 | bytes 180224 | tf_op jit(solution)/shard_map/ijc,cd->ijd/dot_general | solution.py:18
  1.8 0.4 copy.39
  2.3 1.1 %reshape.28 = bf16[4,2,4608]{2,1,0:T(2,128)(2,1)} reshape(bf16[128,12,24]{2,1,0:T(8,128)(2,1)S(1)} %bitcast.44) | data formatting | bytes 147456
  3.4 0.0 copy-start.1
  3.4 5.3 %all-to-all-start = ((bf16[4,2,4608]{2,1,0:T(2,128)(2,1)}), bf16[4,2,4608]{2,1,0:T(2,128)(2,1)S(1)}, u32[]{:S(2)}, u32[]{:S(2)}) async-start(bf16[4,2,4608]{2,1,0:T(2,128)(2,1)} %reshape.28), calls=%async_computation | async-start | bytes 147456 | tf_op jit(solution)/shard_map/all_to_all | solution.py:38
  8.7 0.0 copy-done.1
  8.7 0.2 convolution_convert_fusion
  8.9 0.4 copy.41
  9.3 1.1 %reshape.26 = bf16[4,2,4608]{2,1,0:T(2,128)(2,1)} reshape(bf16[128,12,24]{2,1,0:T(8,128)(2,1)S(1)} %bitcast.45) | data formatting | bytes 147456
  10.5 3.1 %all-to-all-done = bf16[4,2,4608]{2,1,0:T(2,128)(2,1)S(1)} async-done(((bf16[4,2,4608]{2,1,0:T(2,128)(2,1)}), bf16[4,2,4608]{2,1,0:T(2,128)(2,1)S(1)}, u32[]{:S(2)}, u32[]{:S(2)}) %all-to-all-start) | async-done | bytes 73760 | tf_op jit(solution)/shard_map/all_to_all | solution.py:38
  13.6 3.3 %all-to-all-start.1 = ((bf16[4,2,4608]{2,1,0:T(2,128)(2,1)}), bf16[4,2,4608]{2,1,0:T(2,128)(2,1)S(1)}, u32[]{:S(2)}, u32[]{:S(2)}) async-start(bf16[4,2,4608]{2,1,0:T(2,128)(2,1)} %reshape.26), calls=%async_computation.1 | async-start | bytes 147456 | tf_op jit(solution)/shard_map/all_to_all | solution.py:37
  16.9 0.6 %reshape.29 = bf16[128,12,24]{2,1,0:T(8,128)(2,1)S(1)} reshape(bf16[4,2,4608]{2,1,0:T(2,128)(2,1)S(1)} %all-to-all-done) | data formatting | bytes 147456
  17.5 0.3 copy.55
  17.8 0.2 all_to_all.36
  18.0 3.7 %all-to-all-done.1 = bf16[4,2,4608]{2,1,0:T(2,128)(2,1)S(1)} async-done(((bf16[4,2,4608]{2,1,0:T(2,128)(2,1)}), bf16[4,2,4608]{2,1,0:T(2,128)(2,1)S(1)}, u32[]{:S(2)}, u32[]{:S(2)}) %all-to-all-start.1) | async-done | bytes 73760 | tf_op jit(solution)/shard_map/all_to_all | solution.py:37
  21.7 0.6 %reshape.27 = bf16[128,12,24]{2,1,0:T(8,128)(2,1)S(1)} reshape(bf16[4,2,4608]{2,1,0:T(2,128)(2,1)S(1)} %all-to-all-done.1) | data formatting | bytes 147456
  22.3 0.3 copy.54
  22.6 0.2 all_to_all.40
  22.9 16.5 %all_gather.3 = bf16[96,96,32]{0,2,1:T(8,128)(2,1)S(1)} all-gather(bf16[96,12,32]{0,2,1:T(8,128)(2,1)S(1)} %all_to_all.40), channel_id=1, replica_groups=mesh['pr'=4,'pc'=8] {'pc'}, dimensions={1}, use_global_device_ids=true | all-gather | bytes 663552 | tf_op jit(solution)/shard_map/all_gather | solution.py:42
  39.4 0.5 fusion.5
  39.9 0.4 copy.45
  40.3 0.3 reshape.30
  40.6 7.2 %all_to_all.45 = bf16[4,2,4608]{2,1,0:T(2,128)(2,1)S(1)} all-to-all(bf16[4,2,4608]{2,1,0:T(2,128)(2,1)S(1)} %reshape.30), channel_id=1, replica_groups=mesh['pr'=4,'pc'=8] {'pr'}, dimensions={0} | all-to-all | bytes 147456 | tf_op jit(solution)/shard_map/all_to_all | solution.py:47
  47.8 0.2 reshape.31
  48.1 0.3 copy.46
  48.4 0.4 reshape.21
  48.8 0.1 bitcast_reduce_fusion
  48.9 0.3 multiply_reduce_fusion
  49.2 0.3 copy.47
  49.5 0.0 copy-start.3
  49.5 0.3 reshape.19
  49.8 0.4 copy-done.3
  50.2 0.0 copy-start.2
  50.2 0.1 multiply_convert_fusion
  50.3 0.6 %copy-done.2 = bf16[128,128]{1,0:T(8,128)(2,1)S(1)} copy-done((bf16[128,128]{1,0:T(8,128)(2,1)S(1)}, bf16[128,128]{1,0:T(8,128)(2,1)}, u32[]{:S(2)}) %copy-start.2) | copy-done | bytes 32792
  50.9 0.0 copy-start.4
  50.9 0.2 fusion.10
  51.1 0.6 %copy-done.4 = bf16[128,128]{1,0:T(8,128)(2,1)S(1)} copy-done((bf16[128,128]{1,0:T(8,128)(2,1)S(1)}, bf16[128,128]{1,0:T(8,128)(2,1)}, u32[]{:S(2)}) %copy-start.4) | copy-done | bytes 32792
  51.7 0.8 %fusion.6 = bf16[24,12,128]{2,0,1:T(8,128)(2,1)} fusion(f32[24,12,128]{2,0,1:T(8,128)S(1)} %fusion.10, bf16[24,12,128]{2,0,1:T(8,128)(2,1)S(1)} %copy-done, bf16[128,128]{1,0:T(8,128)(2,1)S(1)} %copy-done.4), kind=kOutput, calls=%fused_computation.8 | convolution fusion | flops 9621504 | bytes 327680 | tf_op jit(solution)/shard_map/ijc,cd->ijd/dot_general | solution.py:26
  (2 shorter events, 0.0 us)
Async XLA Ops:
  0.0 0.9 %copy-start = (bf16[24,12,128]{2,0,1:T(8,128)(2,1)S(1)}, bf16[24,12,128]{2,0,1:T(8,128)(2,1)}, u32[]{:S(2)}) copy-start(bf16[24,12,128]{2,0,1:T(8,128)(2,1)} %param.6) | copy-start | bytes 221188
  3.4 5.3 %copy-start.1 = (bf16[128,128]{1,0:T(8,128)(2,1)S(1)}, bf16[128,128]{1,0:T(8,128)(2,1)}, u32[]{:S(2)}) copy-start(bf16[128,128]{1,0:T(8,128)(2,1)} %param.7) | copy-start | bytes 98308
  3.4 10.2 %all-to-all-start = ((bf16[4,2,4608]{2,1,0:T(2,128)(2,1)}), bf16[4,2,4608]{2,1,0:T(2,128)(2,1)S(1)}, u32[]{:S(2)}, u32[]{:S(2)}) async-start(bf16[4,2,4608]{2,1,0:T(2,128)(2,1)} %reshape.28), calls=%async_computation | async-start | bytes 147456 | tf_op jit(solution)/shard_map/all_to_all | solution.py:38
  13.6 8.1 %all-to-all-start.1 = ((bf16[4,2,4608]{2,1,0:T(2,128)(2,1)}), bf16[4,2,4608]{2,1,0:T(2,128)(2,1)S(1)}, u32[]{:S(2)}, u32[]{:S(2)}) async-start(bf16[4,2,4608]{2,1,0:T(2,128)(2,1)} %reshape.26), calls=%async_computation.1 | async-start | bytes 147456 | tf_op jit(solution)/shard_map/all_to_all | solution.py:37
  49.5 0.7 %copy-start.3 = (f32[128]{0:T(128)S(1)}, f32[128]{0:T(128)}, u32[]{:S(2)}) copy-start(f32[128]{0:T(128)} %param.9) | copy-start | bytes 1540
  50.2 0.8 %copy-start.2 = (bf16[128,128]{1,0:T(8,128)(2,1)S(1)}, bf16[128,128]{1,0:T(8,128)(2,1)}, u32[]{:S(2)}) copy-start(bf16[128,128]{1,0:T(8,128)(2,1)} %param.10) | copy-start | bytes 98308
  50.9 0.8 %copy-start.4 = (bf16[128,128]{1,0:T(8,128)(2,1)S(1)}, bf16[128,128]{1,0:T(8,128)(2,1)}, u32[]{:S(2)}) copy-start(bf16[128,128]{1,0:T(8,128)(2,1)} %param.11) | copy-start | bytes 98308
where the time goes:
time: 53.2 us; the launch traced here: 52.5 us
  blocking collectives  23.7 us (45%)
  local copies, waits for them, and re-layouts  10.1 us (19%)
  starting transfers between devices  8.61 us (16%)
  waiting for transfers between devices  6.78 us (13%)
  matrix products  2.61 us (5%)
  other arithmetic  0.54 us (1%)
    all_gather x1, blocking collectives, body(): lax.all_gather(left_lines, 'pc', axis=1, tiled=True)  16.5 us
    all_to_all x1, blocking collectives, body(): mixed = lax.all_to_all(strip, 'pr', split_axis=0, concat_axis=2, tiled=True)  7.24 us
    unnamed x16, local copies, waits for them, and re-layouts  6.51 us
    all_to_all x1, starting transfers between devices, body(): lax.all_to_all(right, 'pr', split_axis=2, concat_axis=0, tiled=True)  5.32 us
    all_to_all x1, waiting for transfers between devices, body(): lax.all_to_all(left, 'pr', split_axis=2, concat_axis=0, tiled=True)  3.68 us
    all_to_all x1, starting transfers between devices, body(): lax.all_to_all(left, 'pr', split_axis=2, concat_axis=0, tiled=True)  3.29 us
    all_to_all x1, waiting for transfers between devices, body(): lax.all_to_all(right, 'pr', split_axis=2, concat_axis=0, tiled=True)  3.1 us
  transfers between devices with their start and end apart: 2, of which 2 were waited for; matrix products, arithmetic and copies ran while one was open for 5% of the time, Pallas kernels for 0%

commit v1 on v0

--- a/solution.py
+++ b/solution.py
@@ -37,11 +37,30 @@
         lax.all_to_all(left, "pr", split_axis=2, concat_axis=0, tiled=True),
         lax.all_to_all(right, "pr", split_axis=2, concat_axis=0, tiled=True),
     )
-    strip = jnp.einsum(
-        "kid,kjd->ijd",
-        lax.all_gather(left_lines, "pc", axis=1, tiled=True),
-        right_lines,
-        preferred_element_type=jnp.float32,
+
+    def create_desk(page, t0):
+        state_now = lax.axis_size("pc")
+        current_value, t1, seen_now = (state_now, lax.axis_index("pc"), page.shape[1])
+        frames = []
+        for i0 in tuple(range(current_value)):
+            arr_now = (
+                lax.ppermute(
+                    page, "pc", [(c, (c + 1) % current_value) for c in range(current_value)]
+                )
+                if i0 + 1 < current_value
+                else page
+            )
+            carry = t0(page, (t1 - i0) % current_value * seen_now)
+            frames.append(carry)
+            page = arr_now
+        before = jnp.concatenate(frames[::-1], axis=0)
+        return jnp.roll(before, shift=(t1 + 1) * frames[0].shape[0], axis=0)
+
+    strip = create_desk(
+        left_lines,
+        lambda part, at: jnp.einsum(
+            "kid,kjd->ijd", part, right_lines, preferred_element_type=jnp.float32
+        ),
     )
     strip = (strip * count ** (-0.5)).astype(jnp.bfloat16)
     mixed = lax.all_to_all(strip, "pr", split_axis=0, concat_axis=2, tiled=True)

time: 53.2 us -> 77.9 us (1.46)
  waiting for transfers between devices: 6.78 us -> 43.4 us
  blocking collectives: 23.7 us -> 8.8 us
  local copies, waits for them, and re-layouts: 10.1 us -> 11.8 us
  matrix products: 2.61 us -> 3.5 us
    ppermute x0 -> x7, waiting for transfers between devices: none -> 36.8 us  [create_desk(): lax.ppermute(page, 'pc', [(c, (c + 1) % current_value) for c in range(cur...]
    all_gather x1 -> x0, blocking collectives: 16.5 us -> none  [body(): lax.all_gather(left_lines, 'pc', axis=1, tiled=True)]
    all_to_all x1, starting transfers between devices: 5.32 us -> 3.29 us  [body(): lax.all_to_all(right, 'pr', split_axis=2, concat_axis=0, tiled=True)]
    all_to_all x1, starting transfers between devices: 3.29 us -> 5.32 us  [body(): lax.all_to_all(left, 'pr', split_axis=2, concat_axis=0, tiled=True)]
    all_to_all x1, blocking collectives: 7.24 us -> 8.8 us  [body(): mixed = lax.all_to_all(strip, 'pr', split_axis=0, concat_axis=2, tiled=True)]
    concatenate x0 -> x1, local copies, waits for them, and re-layouts: none -> 1.19 us  [create_desk(): return jnp.roll(before, shift=(t1 + 1) * frames[0].shape[0], axis=0)]
    dot_general x1 -> x8, matrix products: 0.52 us -> 1.4 us  [body(): jnp.einsum('kid,kjd->ijd', part, right_lines, preferred_element_type=jnp....]
  transfers between devices with their start and end apart: 2 -> 9, of which waited for: 2 -> 9; matrix products, arithmetic and copies ran while one was open for 5% -> 7% of each run, Pallas kernels for 0% -> 0%
where the time goes in v1:
time: 77.9 us; the launch traced here: 77.3 us
  waiting for transfers between devices  43.4 us (56%)
  local copies, waits for them, and re-layouts  11.8 us (15%)
  blocking collectives  8.8 us (11%)
  starting transfers between devices  8.68 us (11%)
  matrix products  3.5 us (4%)
    ppermute x7, waiting for transfers between devices, create_desk(): lax.ppermute(page, 'pc', [(c, (c + 1) % current_value) for c in range(cur...  36.8 us
    all_to_all x1, blocking collectives, body(): mixed = lax.all_to_all(strip, 'pr', split_axis=0, concat_axis=2, tiled=True)  8.8 us
    unnamed x16, local copies, waits for them, and re-layouts  6.51 us
    all_to_all x1, starting transfers between devices, body(): lax.all_to_all(left, 'pr', split_axis=2, concat_axis=0, tiled=True)  5.32 us
    all_to_all x1, waiting for transfers between devices, body(): lax.all_to_all(right, 'pr', split_axis=2, concat_axis=0, tiled=True)  3.54 us
    all_to_all x1, starting transfers between devices, body(): lax.all_to_all(right, 'pr', split_axis=2, concat_axis=0, tiled=True)  3.29 us
    all_to_all x1, waiting for transfers between devices, body(): lax.all_to_all(left, 'pr', split_axis=2, concat_axis=0, tiled=True)  3.11 us
  transfers between devices with their start and end apart: 9, of which 9 were waited for; matrix products, arithmetic and copies ran while one was open for 7% of the time, Pallas kernels for 0%

profile of v1, /device:TPU:0, one launch (start us, length us, event | category | flops | bytes accessed | tf_op | source)
XLA Modules:
  0.0 77.3 jit_solution(11154329653775245327)
XLA Ops:
  0.0 0.9 %copy-done = bf16[24,12,128]{2,0,1:T(8,128)(2,1)S(1)} copy-done((bf16[24,12,128]{2,0,1:T(8,128)(2,1)S(1)}, bf16[24,12,128]{2,0,1:T(8,128)(2,1)}, u32[]{:S(2)}) %copy-start) | copy-done | bytes 73752
  0.9 0.9 %convolution_convert_fusion = bf16[24,12,128]{2,0,1:T(8,128)(2,1)S(1)} fusion(bf16[24,12,128]{2,0,1:T(8,128)(2,1)S(1)} %copy-done, bf16[128,128]{1,0:T(8,128)(2,1)} %param.7), kind=kOutput, calls=%fused_computation.6 | convolution fusion | flops 9474048 | bytes 180224 | tf_op jit(solution)/shard_map/ijc,cd->ijd/dot_general | solution.py:17
  1.8 0.4 copy.73
  2.3 1.1 %reshape.26 = bf16[4,2,4608]{2,1,0:T(2,128)(2,1)} reshape(bf16[128,12,24]{2,1,0:T(8,128)(2,1)S(1)} %bitcast.73) | data formatting | bytes 147456
  3.4 5.3 %all-to-all-start.1 = ((bf16[4,2,4608]{2,1,0:T(2,128)(2,1)}), bf16[4,2,4608]{2,1,0:T(2,128)(2,1)S(1)}, u32[]{:S(2)}, u32[]{:S(2)}) async-start(bf16[4,2,4608]{2,1,0:T(2,128)(2,1)} %reshape.26), calls=%async_computation.1 | async-start | bytes 147456 | tf_op jit(solution)/shard_map/all_to_all | solution.py:37
  8.7 0.2 convolution_convert_fusion.1
  8.9 0.4 copy.71
  9.4 1.1 %reshape.28 = bf16[4,2,4608]{2,1,0:T(2,128)(2,1)} reshape(bf16[128,12,24]{2,1,0:T(8,128)(2,1)S(1)} %bitcast.74) | data formatting | bytes 147456
  10.5 3.1 %all-to-all-done.1 = bf16[4,2,4608]{2,1,0:T(2,128)(2,1)S(1)} async-done(((bf16[4,2,4608]{2,1,0:T(2,128)(2,1)}), bf16[4,2,4608]{2,1,0:T(2,128)(2,1)S(1)}, u32[]{:S(2)}, u32[]{:S(2)}) %all-to-all-start.1) | async-done | bytes 73760 | tf_op jit(solution)/shard_map/all_to_all | solution.py:37
  13.6 3.3 %all-to-all-start = ((bf16[4,2,4608]{2,1,0:T(2,128)(2,1)}), bf16[4,2,4608]{2,1,0:T(2,128)(2,1)S(1)}, u32[]{:S(2)}, u32[]{:S(2)}) async-start(bf16[4,2,4608]{2,1,0:T(2,128)(2,1)} %reshape.28), calls=%async_computation | async-start | bytes 147456 | tf_op jit(solution)/shard_map/all_to_all | solution.py:38
  16.9 0.6 reshape.27
  17.5 0.3 copy.124
  17.8 0.2 all_to_all.40
  18.2 3.5 %all-to-all-done = bf16[4,2,4608]{2,1,0:T(2,128)(2,1)S(1)} async-done(((bf16[4,2,4608]{2,1,0:T(2,128)(2,1)}), bf16[4,2,4608]{2,1,0:T(2,128)(2,1)S(1)}, u32[]{:S(2)}, u32[]{:S(2)}) %all-to-all-start) | async-done | bytes 73760 | tf_op jit(solution)/shard_map/all_to_all | solution.py:38
  21.7 0.6 reshape.29
  22.3 0.3 copy.125
  22.7 0.2 all_to_all.36
  22.9 0.2 fusion.5
  23.1 1.2 %collective-permute-done = bf16[96,12,32]{0,1,2:T(8,128)(2,1)S(1)} collective-permute-done((bf16[96,12,32]{0,1,2:T(8,128)(2,1)S(1)}, bf16[96,12,32]{0,1,2:T(8,128)(2,1)S(1)}, u32[]{:S(2)}, u32[]{:S(2)}) %collective-permute-start) | collective-permute-done | bytes 73760 | tf_op jit(solution)/shard_map/ppermute | solution.py:47
  24.4 0.2 fusion.7
  24.6 5.9 %collective-permute-done.1 = bf16[96,12,32]{0,1,2:T(8,128)(2,1)S(1)} collective-permute-done((bf16[96,12,32]{0,1,2:T(8,128)(2,1)S(1)}, bf16[96,12,32]{0,1,2:T(8,128)(2,1)S(1)}, u32[]{:S(2)}, u32[]{:S(2)}) %collective-permute-start.1) | collective-permute-done | bytes 73760 | tf_op jit(solution)/shard_map/ppermute | solution.py:47
  30.6 0.2 fusion.9
  30.8 5.9 %collective-permute-done.2 = bf16[96,12,32]{0,1,2:T(8,128)(2,1)S(1)} collective-permute-done((bf16[96,12,32]{0,1,2:T(8,128)(2,1)S(1)}, bf16[96,12,32]{0,1,2:T(8,128)(2,1)S(1)}, u32[]{:S(2)}, u32[]{:S(2)}) %collective-permute-start.2) | collective-permute-done | bytes 73760 | tf_op jit(solution)/shard_map/ppermute | solution.py:47
  36.8 0.2 fusion.11
  37.0 5.9 %collective-permute-done.3 = bf16[96,12,32]{0,1,2:T(8,128)(2,1)S(1)} collective-permute-done((bf16[96,12,32]{0,1,2:T(8,128)(2,1)S(1)}, bf16[96,12,32]{0,1,2:T(8,128)(2,1)S(1)}, u32[]{:S(2)}, u32[]{:S(2)}) %collective-permute-start.3) | collective-permute-done | bytes 73760 | tf_op jit(solution)/shard_map/ppermute | solution.py:47
  43.0 0.2 fusion.13
  43.2 5.9 %collective-permute-done.4 = bf16[96,12,32]{0,1,2:T(8,128)(2,1)S(1)} collective-permute-done((bf16[96,12,32]{0,1,2:T(8,128)(2,1)S(1)}, bf16[96,12,32]{0,1,2:T(8,128)(2,1)S(1)}, u32[]{:S(2)}, u32[]{:S(2)}) %collective-permute-start.4) | collective-permute-done | bytes 73760 | tf_op jit(solution)/shard_map/ppermute | solution.py:47
  49.1 0.2 fusion.15
  49.4 5.9 %collective-permute-done.5 = bf16[96,12,32]{0,1,2:T(8,128)(2,1)S(1)} collective-permute-done((bf16[96,12,32]{0,1,2:T(8,128)(2,1)S(1)}, bf16[96,12,32]{0,1,2:T(8,128)(2,1)S(1)}, u32[]{:S(2)}, u32[]{:S(2)}) %collective-permute-start.5) | collective-permute-done | bytes 73760 | tf_op jit(solution)/shard_map/ppermute | solution.py:47
  55.3 0.2 fusion.17
  55.6 5.9 %collective-permute-done.6 = bf16[96,12,32]{0,1,2:T(8,128)(2,1)S(1)} collective-permute-done((bf16[96,12,32]{0,1,2:T(8,128)(2,1)S(1)}, bf16[96,12,32]{0,1,2:T(8,128)(2,1)S(1)}, u32[]{:S(2)}, u32[]{:S(2)}) %collective-permute-start.6) | collective-permute-done | bytes 73760 | tf_op jit(solution)/shard_map/ppermute | solution.py:47
  61.5 0.2 fusion.19
  61.8 1.2 %concatenate.6 = f32[192,12,32]{0,2,1:T(8,128)S(1)} concatenate(f32[12,12,32]{0,2,1:T(8,128)S(1)} %bitcast.89, f32[12,12,32]{0,2,1:T(8,128)S(1)} %bitcast.87, f32[12,12,32]{0,2,1:T(8,128)S(1)} %bitcast.85, f32[12,12,32]{0,2,1:T(8,128)S(1)} %bitcast.83, f32[12,12,32]{0,2,1:T(8,128)S(1)} %bitcast.81, f32[12,12,32]{0,2,1:T(8,128)S(1)} %bitcast.79, f32[12,12,32]{0,2,1:T(8,128)S(1)} %bitcast.77, ...), dimensions={0} | concatenate | bytes 589824 | tf_op jit(solution)/shard_map/jit(_roll_dynamic)/concatenate | solution.py:57
  63.1 0.3 copy.93
  63.5 0.3 reshape.30
  63.8 8.8 %all_to_all.45 = bf16[4,2,4608]{2,1,0:T(2,128)(2,1)S(1)} all-to-all(bf16[4,2,4608]{2,1,0:T(2,128)(2,1)S(1)} %reshape.30), channel_id=1, replica_groups=mesh['pr'=4,'pc'=8] {'pr'}, dimensions={0} | all-to-all | bytes 147456 | tf_op jit(solution)/shard_map/all_to_all | solution.py:66
  72.6 0.2 reshape.31
  72.8 0.3 copy.94
  73.1 0.4 reshape.21
  73.7 0.3 multiply_reduce_fusion
  73.9 0.3 copy.95
  74.3 0.3 reshape.19
  74.6 0.4 copy-done.3
  74.9 0.1 multiply_convert_fusion.1
  75.1 0.6 copy-done.2
  75.7 0.2 fusion.22
  75.8 0.6 copy-done.4
  76.4 0.8 %fusion.4 = bf16[24,12,128]{2,0,1:T(8,128)(2,1)} fusion(f32[24,12,128]{2,0,1:T(8,128)S(1)} %fusion.22, bf16[24,12,128]{2,0,1:T(8,128)(2,1)S(1)} %copy-done, bf16[128,128]{1,0:T(8,128)(2,1)S(1)} %copy-done.4), kind=kOutput, calls=%fused_computation.5 | convolution fusion | flops 9621504 | bytes 327680 | tf_op jit(solution)/shard_map/ijc,cd->ijd/dot_general | solution.py:26
  (26 shorter events, 1.0 us)
Async XLA Ops:
  0.0 0.9 %copy-start = (bf16[24,12,128]{2,0,1:T(8,128)(2,1)S(1)}, bf16[24,12,128]{2,0,1:T(8,128)(2,1)}, u32[]{:S(2)}) copy-start(bf16[24,12,128]{2,0,1:T(8,128)(2,1)} %param.6) | copy-start | bytes 221188
  3.4 5.3 %copy-start.1 = (bf16[128,128]{1,0:T(8,128)(2,1)S(1)}, bf16[128,128]{1,0:T(8,128)(2,1)}, u32[]{:S(2)}) copy-start(bf16[128,128]{1,0:T(8,128)(2,1)} %param.8) | copy-start | bytes 98308
  3.4 10.2 %all-to-all-start.1 = ((bf16[4,2,4608]{2,1,0:T(2,128)(2,1)}), bf16[4,2,4608]{2,1,0:T(2,128)(2,1)S(1)}, u32[]{:S(2)}, u32[]{:S(2)}) async-start(bf16[4,2,4608]{2,1,0:T(2,128)(2,1)} %reshape.26), calls=%async_computation.1 | async-start | bytes 147456 | tf_op jit(solution)/shard_map/all_to_all | solution.py:37
  13.6 8.1 %all-to-all-start = ((bf16[4,2,4608]{2,1,0:T(2,128)(2,1)}), bf16[4,2,4608]{2,1,0:T(2,128)(2,1)S(1)}, u32[]{:S(2)}, u32[]{:S(2)}) async-start(bf16[4,2,4608]{2,1,0:T(2,128)(2,1)} %reshape.28), calls=%async_computation | async-start | bytes 147456 | tf_op jit(solution)/shard_map/all_to_all | solution.py:38
  18.1 6.2 %collective-permute-start = (bf16[96,12,32]{0,1,2:T(8,128)(2,1)S(1)}, bf16[96,12,32]{0,1,2:T(8,128)(2,1)S(1)}, u32[]{:S(2)}, u32[]{:S(2)}) collective-permute-start(bf16[96,12,32]{0,1,2:T(8,128)(2,1)S(1)} %copy.75), channel_id=1, source_target_pairs={{0,1},{1,2},{2,3},{3,4},{4,5},{5,6},{6,7},{7,0},{8,9},{9,10},{10,1... | collective-permute-start | bytes 221192 | tf_op jit(solution)/shard_map/ppermute | solution.py:47
  24.4 6.2 %collective-permute-start.1 = (bf16[96,12,32]{0,1,2:T(8,128)(2,1)S(1)}, bf16[96,12,32]{0,1,2:T(8,128)(2,1)S(1)}, u32[]{:S(2)}, u32[]{:S(2)}) collective-permute-start(bf16[96,12,32]{0,1,2:T(8,128)(2,1)S(1)} %collective-permute-done), channel_id=1, source_target_pairs={{0,1},{1,2},{2,3},{3,4},{4,5},{5,6},{6,7},{7,0},{8,9},{9,10},{10,1... | collective-permute-start | bytes 221192 | tf_op jit(solution)/shard_map/ppermute | solution.py:47
  30.6 6.2 %collective-permute-start.2 = (bf16[96,12,32]{0,1,2:T(8,128)(2,1)S(1)}, bf16[96,12,32]{0,1,2:T(8,128)(2,1)S(1)}, u32[]{:S(2)}, u32[]{:S(2)}) collective-permute-start(bf16[96,12,32]{0,1,2:T(8,128)(2,1)S(1)} %collective-permute-done.1), channel_id=1, source_target_pairs={{0,1},{1,2},{2,3},{3,4},{4,5},{5,6},{6,7},{7,0},{8,9},{9,10},{10,1... | collective-permute-start | bytes 221192 | tf_op jit(solution)/shard_map/ppermute | solution.py:47
  36.8 6.2 %collective-permute-start.3 = (bf16[96,12,32]{0,1,2:T(8,128)(2,1)S(1)}, bf16[96,12,32]{0,1,2:T(8,128)(2,1)S(1)}, u32[]{:S(2)}, u32[]{:S(2)}) collective-permute-start(bf16[96,12,32]{0,1,2:T(8,128)(2,1)S(1)} %collective-permute-done.2), channel_id=1, source_target_pairs={{0,1},{1,2},{2,3},{3,4},{4,5},{5,6},{6,7},{7,0},{8,9},{9,10},{10,1... | collective-permute-start | bytes 221192 | tf_op jit(solution)/shard_map/ppermute | solution.py:47
  42.9 6.2 %collective-permute-start.4 = (bf16[96,12,32]{0,1,2:T(8,128)(2,1)S(1)}, bf16[96,12,32]{0,1,2:T(8,128)(2,1)S(1)}, u32[]{:S(2)}, u32[]{:S(2)}) collective-permute-start(bf16[96,12,32]{0,1,2:T(8,128)(2,1)S(1)} %collective-permute-done.3), channel_id=1, source_target_pairs={{0,1},{1,2},{2,3},{3,4},{4,5},{5,6},{6,7},{7,0},{8,9},{9,10},{10,1... | collective-permute-start | bytes 221192 | tf_op jit(solution)/shard_map/ppermute | solution.py:47
  49.1 6.2 %collective-permute-start.5 = (bf16[96,12,32]{0,1,2:T(8,128)(2,1)S(1)}, bf16[96,12,32]{0,1,2:T(8,128)(2,1)S(1)}, u32[]{:S(2)}, u32[]{:S(2)}) collective-permute-start(bf16[96,12,32]{0,1,2:T(8,128)(2,1)S(1)} %collective-permute-done.4), channel_id=1, source_target_pairs={{0,1},{1,2},{2,3},{3,4},{4,5},{5,6},{6,7},{7,0},{8,9},{9,10},{10,1... | collective-permute-start | bytes 221192 | tf_op jit(solution)/shard_map/ppermute | solution.py:47
  55.3 6.2 %collective-permute-start.6 = (bf16[96,12,32]{0,1,2:T(8,128)(2,1)S(1)}, bf16[96,12,32]{0,1,2:T(8,128)(2,1)S(1)}, u32[]{:S(2)}, u32[]{:S(2)}) collective-permute-start(bf16[96,12,32]{0,1,2:T(8,128)(2,1)S(1)} %collective-permute-done.5), channel_id=1, source_target_pairs={{0,1},{1,2},{2,3},{3,4},{4,5},{5,6},{6,7},{7,0},{8,9},{9,10},{10,1... | collective-permute-start | bytes 221192 | tf_op jit(solution)/shard_map/ppermute | solution.py:47
  74.3 0.7 copy-start.3
  74.9 0.8 copy-start.2
  75.7 0.8 copy-start.4
